TPU v7x, 32 devices: a whole 2x2x4 slice. The times are simulated.
32 devices in a mesh: section: 2 (over core), dp: 16 (over z, y, x).
Axes of the slice: x: 2, y: 2, z: 4, core: 2. Of those that a mesh axis runs over, the one named last changes fastest.
Arguments:
- ends: bfloat16 [2, 2, 96, 256, 384], P('section', None, 'dp'), may hold values from -6 to 6
- counts: int32 [2, 16], P(None, 'dp'), may hold values from 1 to 6, as said below
- qkv_weight: bfloat16 [2, 384, 1152], P('section', 'dp'), may hold values from -0.3125 to 0.3125
- out_weight: bfloat16 [2, 384, 384], P('section', 'dp'), may hold values from -1.25 to 1.25
- up_weight: bfloat16 [2, 384, 1536], P('section', 'dp'), may hold values from -0.3125 to 0.3125
- down_weight: bfloat16 [2, 1536, 384], P('section', 'dp'), may hold values from -0.15625 to 0.15625
- norm_gains: bfloat16 [2, 2, 384], P('section', None, 'dp'), may hold values from 0.5 to 1.5
- norm_shifts: bfloat16 [2, 2, 384], P('section', None, 'dp'), may hold values from -3 to 3
- up_bias: bfloat16 [2, 1536], P('section', 'dp'), may hold values from -3 to 3
Outputs:
- ends_out: float32 [2, 2, 96, 256, 384], P('section', None, 'dp')
- qkv_grad: float32 [2, 384, 1152], P('section', 'dp')
- out_grad: float32 [2, 384, 384], P('section', 'dp')
- up_grad: float32 [2, 384, 1536], P('section', 'dp')
- down_grad: float32 [2, 1536, 384], P('section', 'dp')
- gains_grad: float32 [2, 2, 384], P('section', None, 'dp')
- shifts_grad: float32 [2, 2, 384], P('section', None, 'dp')
- up_bias_grad: float32 [2, 1536], P('section', 'dp')
Inputs may be any that keep to these rules, and one draw needn't show every extreme that they name: `counts`: in every micro-batch some dp index runs exactly 6 images.
All inputs are finite; a program needn't handle non-finite values.
Results may differ from a plain program's by a relative error of at most 0.0089.
Values may be sent and summed in bfloat16 or wider, within the bound.
A program may use at most 256 MiB of HBM per device.

v0:
```python
import math

import jax
import jax.numpy as jnp
from jax import lax
from jax.sharding import PartitionSpec as P

H = 6
HD = 64
PAD = 256
SEQ = 197


EPS = 1e-06
SQRT_HALF = 0.7071067811865476
INV_ROOT_TWO_PI = 0.3989422804014327


def shifted_2(value, axis, steps):
    count = lax.axis_size(axis)
    first, last = (max(0, -steps), min(count, count - steps))
    return lax.ppermute(value, axis, [(source, source + steps) for source in range(first, last)])


def split_up(array, dim, length):
    before, after = (array.shape[:dim], array.shape[dim + 1 :])
    return jnp.moveaxis(array.reshape(*before, length, -1, *after), dim, 0)


def sum_at_owner(array, axis, dim):
    parts = split_up(array, dim, lax.axis_size(axis))
    arrived = lax.all_to_all(parts, axis, split_axis=0, concat_axis=0, tiled=True)
    return arrived.astype(jnp.float32).sum(axis=0)


def side_by_side(arrays, axis, dim, along):
    ends, at = ([], 0)
    for a in arrays[:-1]:
        at += a.shape[along]
        ends.append(at)
    both = jnp.concatenate(arrays, axis=along)
    return tuple(jnp.split(sum_at_owner(both, axis, dim), ends, axis=along))


def normalize(values, gain, shift):
    centred = values - jnp.mean(values, -1, keepdims=True)
    inverse = lax.rsqrt(jnp.mean(centred * centred, -1, keepdims=True) + EPS)
    normed = centred * inverse
    return (normed * gain + shift, normed, inverse)


def norm_back(grad_out, normed, inverse, gain):
    scaled = grad_out * gain
    grad_in = inverse * (
        scaled
        - jnp.mean(scaled, -1, keepdims=True)
        - normed * jnp.mean(scaled * normed, -1, keepdims=True)
    )
    return (grad_in, jnp.sum(grad_out * normed, 0), jnp.sum(grad_out, 0))


def run_layer(layer_in, weights):
    w_qkv, w_out, w_up, w_down, gain_rows, shift_rows, up_shift = weights
    gain_rows = gain_rows.astype(jnp.float32)
    shift_rows = shift_rows.astype(jnp.float32)
    row_count = layer_in.shape[0]
    image_count = row_count // PAD
    normed_in, unit_one, inverse_one = normalize(layer_in, gain_rows[0], shift_rows[0])
    normed_low = normed_in.astype(jnp.bfloat16)
    packed = jnp.dot(normed_low, w_qkv, preferred_element_type=jnp.float32).astype(jnp.bfloat16)
    packed = packed.reshape(image_count, PAD, 3, H, HD)
    query_heads = packed[:, :, 0]
    key_heads = packed[:, :, 1]
    value_heads = packed[:, :, 2]
    scale = 1.0 / math.sqrt(HD)
    scores = (
        jnp.einsum("bqhd,bkhd->bhqk", query_heads, key_heads, preferred_element_type=jnp.float32)
        * scale
    )
    token_valid = lax.iota(jnp.int32, PAD) < SEQ
    scores = jnp.where(token_valid, scores, -1e30)
    shifted = jnp.exp(scores - jnp.max(scores, -1, keepdims=True))
    soft = shifted / jnp.sum(shifted, -1, keepdims=True)
    soft_low = soft.astype(jnp.bfloat16)
    attended = jnp.einsum(
        "bhqk,bkhd->bqhd", soft_low, value_heads, preferred_element_type=jnp.float32
    )
    attended = attended.reshape(row_count, H * HD).astype(jnp.bfloat16)
    middle = layer_in + jnp.dot(attended, w_out, preferred_element_type=jnp.float32)
    normed_mid, unit_two, inverse_two = normalize(middle, gain_rows[1], shift_rows[1])
    mid_low = normed_mid.astype(jnp.bfloat16)
    pre_act = jnp.dot(mid_low, w_up, preferred_element_type=jnp.float32) + up_shift.astype(
        jnp.float32
    )
    hidden = jax.nn.gelu(pre_act, approximate=False).astype(jnp.bfloat16)
    result = middle + jnp.dot(hidden, w_down, preferred_element_type=jnp.float32)
    kept_state = (
        unit_one,
        inverse_one,
        normed_low,
        query_heads,
        key_heads,
        value_heads,
        soft,
        soft_low,
        attended,
        unit_two,
        inverse_two,
        mid_low,
        pre_act,
        hidden,
    )
    return (result, kept_state)


def back_layer(grad_out, kept_state, weights):
    w_qkv, w_out, w_up, w_down, gain_rows, shift_rows, up_shift = weights
    gain_rows = gain_rows.astype(jnp.float32)
    (
        unit_one,
        inverse_one,
        normed_low,
        query_heads,
        key_heads,
        value_heads,
        soft,
        soft_low,
        attended,
        unit_two,
        inverse_two,
        mid_low,
        pre_act,
        hidden,
    ) = kept_state
    row_count = grad_out.shape[0]
    image_count = row_count // PAD
    grad_down = grad_out.astype(jnp.bfloat16)
    d_down = jnp.dot(hidden.T, grad_down, preferred_element_type=jnp.float32)
    grad_hidden = jnp.dot(grad_down, w_down.T, preferred_element_type=jnp.float32)
    slope = (
        0.5 * (1.0 + lax.erf(pre_act * SQRT_HALF))
        + pre_act * jnp.exp(-0.5 * pre_act * pre_act) * INV_ROOT_TWO_PI
    )
    grad_pre = (grad_hidden * slope).astype(jnp.bfloat16)
    d_up = jnp.dot(mid_low.T, grad_pre, preferred_element_type=jnp.float32)
    d_up_shift = jnp.sum(grad_pre.astype(jnp.float32), 0)
    grad_mid_norm = jnp.dot(grad_pre, w_up.T, preferred_element_type=jnp.float32)
    grad_mid_part, d_gain_two, d_shift_two = norm_back(
        grad_mid_norm, unit_two, inverse_two, gain_rows[1]
    )
    grad_mid = grad_out + grad_mid_part
    grad_branch = grad_mid.astype(jnp.bfloat16)
    d_out = jnp.dot(attended.T, grad_branch, preferred_element_type=jnp.float32)
    grad_att = jnp.dot(grad_branch, w_out.T, preferred_element_type=jnp.float32).astype(
        jnp.bfloat16
    )
    grad_att = grad_att.reshape(image_count, PAD, H, HD)
    d_values = jnp.einsum("bhqk,bqhd->bkhd", soft_low, grad_att, preferred_element_type=jnp.float32)
    grad_soft = jnp.einsum(
        "bqhd,bkhd->bhqk", grad_att, value_heads, preferred_element_type=jnp.float32
    )
    grad_scores = (soft * (grad_soft - jnp.sum(grad_soft * soft, -1, keepdims=True))).astype(
        jnp.bfloat16
    )
    scale = 1.0 / math.sqrt(HD)
    d_query = (
        jnp.einsum("bhqk,bkhd->bqhd", grad_scores, key_heads, preferred_element_type=jnp.float32)
        * scale
    )
    d_keys = (
        jnp.einsum("bhqk,bqhd->bkhd", grad_scores, query_heads, preferred_element_type=jnp.float32)
        * scale
    )
    grad_qkv = (
        jnp.stack([d_query, d_keys, d_values], axis=2)
        .reshape(row_count, 3 * H * HD)
        .astype(jnp.bfloat16)
    )
    d_qkv = jnp.dot(normed_low.T, grad_qkv, preferred_element_type=jnp.float32)
    grad_in_norm = jnp.dot(grad_qkv, w_qkv.T, preferred_element_type=jnp.float32)
    grad_in_part, d_gain_one, d_shift_one = norm_back(
        grad_in_norm, unit_one, inverse_one, gain_rows[0]
    )
    grad_in = grad_mid + grad_in_part
    weight_grads = (
        d_qkv,
        d_out,
        d_up,
        d_down,
        jnp.stack([d_gain_one, d_gain_two]),
        jnp.stack([d_shift_one, d_shift_two]),
        d_up_shift,
    )
    return (grad_in, weight_grads)


def body(
    ends, counts, qkv_weight, out_weight, up_weight, down_weight, norm_gains, norm_shifts, up_bias
):
    is_first = lax.axis_index("section") == 0
    gathered = (
        lax.all_gather(qkv_weight, "dp", axis=1, tiled=True),
        lax.all_gather(out_weight, "dp", axis=1, tiled=True),
        lax.all_gather(up_weight, "dp", axis=1, tiled=True),
        lax.all_gather(down_weight, "dp", axis=1, tiled=True),
        lax.all_gather(norm_gains, "dp", axis=2, tiled=True),
        lax.all_gather(norm_shifts, "dp", axis=2, tiled=True),
        lax.all_gather(up_bias, "dp", axis=1, tiled=True),
    )
    weights = tuple((item[0] for item in gathered))
    micro_count = ends.shape[1]
    slot_count = ends.shape[2]
    row_count = slot_count * ends.shape[3]
    feature_dim = ends.shape[4]
    token_valid = lax.iota(jnp.int32, PAD) < SEQ

    def live_rows(micro_index):
        slot_live = lax.iota(jnp.int32, slot_count) < counts[micro_index, 0]
        both = slot_live[:, None] & token_valid[None, :]
        return both.reshape(row_count, 1).astype(jnp.float32)

    received = jnp.zeros((row_count, feature_dim), jnp.bfloat16)
    saved_states = []
    finals = []
    for step_index in range(micro_count + 1):
        own_rows = ends[0, min(step_index, micro_count - 1)].reshape(row_count, feature_dim)
        layer_in = jnp.where(is_first, own_rows, received)
        result, kept_state = run_layer(layer_in.astype(jnp.float32), weights)
        saved_states.append(kept_state)
        if step_index >= 1:
            finals.append(result * live_rows(step_index - 1))
        if step_index < micro_count:
            received = shifted_2(result.astype(jnp.bfloat16), "section", 1)
    gathered = (
        lax.all_gather(qkv_weight, "dp", axis=1, tiled=True),
        lax.all_gather(out_weight, "dp", axis=1, tiled=True),
        lax.all_gather(up_weight, "dp", axis=1, tiled=True),
        lax.all_gather(down_weight, "dp", axis=1, tiled=True),
        lax.all_gather(norm_gains, "dp", axis=2, tiled=True),
        lax.all_gather(norm_shifts, "dp", axis=2, tiled=True),
        lax.all_gather(up_bias, "dp", axis=1, tiled=True),
    )
    weights = tuple((item[0] for item in gathered))
    received = jnp.zeros((row_count, feature_dim), jnp.bfloat16)
    input_grads = []
    totals = None
    for step_index in range(micro_count + 1):
        micro_index = micro_count - 1 - step_index
        if micro_index >= 0:
            seed_grad = ends[0, micro_index].reshape(row_count, feature_dim).astype(
                jnp.float32
            ) * live_rows(micro_index)
        else:
            seed_grad = jnp.zeros((row_count, feature_dim), jnp.float32)
        grad_out = jnp.where(is_first, received.astype(jnp.float32), seed_grad)
        grad_in, weight_grads = back_layer(
            grad_out, saved_states[micro_count - step_index], weights
        )
        if step_index >= 1:
            input_grads.append(grad_in)
        if step_index < micro_count:
            received = shifted_2(grad_in.astype(jnp.bfloat16), "section", -1)
        if totals is None:
            totals = weight_grads
        else:
            totals = tuple((left + right for left, right in zip(totals, weight_grads)))
    grad_shards = (
        *side_by_side(
            (
                totals[0][None].astype(jnp.bfloat16),
                totals[1][None].astype(jnp.bfloat16),
                totals[2][None].astype(jnp.bfloat16),
            ),
            "dp",
            1,
            2,
        ),
        sum_at_owner(totals[3][None].astype(jnp.bfloat16), "dp", 1),
        *side_by_side(
            (totals[4][None].astype(jnp.bfloat16), totals[5][None].astype(jnp.bfloat16)), "dp", 2, 0
        ),
        sum_at_owner(totals[6][None].astype(jnp.bfloat16), "dp", 1),
    )
    backward_rows = jnp.stack(input_grads[::-1])
    forward_rows = jnp.stack(finals)
    ends_out = jnp.where(is_first, backward_rows, forward_rows).reshape(
        1, micro_count, slot_count, PAD, feature_dim
    )
    return (
        ends_out,
        grad_shards[0],
        grad_shards[1],
        grad_shards[2],
        grad_shards[3],
        grad_shards[4],
        grad_shards[5],
        grad_shards[6],
    )


def solution(mesh):
    in_specs = (
        P("section", None, "dp", None, None),
        P(None, "dp"),
        P("section", "dp", None),
        P("section", "dp", None),
        P("section", "dp", None),
        P("section", "dp", None),
        P("section", None, "dp"),
        P("section", None, "dp"),
        P("section", "dp"),
    )
    out_specs = (
        P("section", None, "dp", None, None),
        P("section", "dp", None),
        P("section", "dp", None),
        P("section", "dp", None),
        P("section", "dp", None),
        P("section", None, "dp"),
        P("section", None, "dp"),
        P("section", "dp"),
    )
    return jax.shard_map(body, mesh=mesh, in_specs=in_specs, out_specs=out_specs, check_vma=False)
```

profile of v0, /device:TPU:0, one launch (start us, length us, event | category | flops | bytes accessed | tf_op | source)
XLA Modules:
  0.0 853.2 jit_solution(13567578367465726931)
XLA Ops:
  17.5 43.8 %all-reduce = bf16[1536]{0:T(1024)(128)(2,1)S(1)} all-reduce(bf16[1536]{0:T(1024)(128)(2,1)S(1)} %dynamic-update-slice), channel_id=1, replica_groups=mesh['section'=2,'dp'=16] {'dp'}, use_global_device_ids=true, to_apply=%add | all-reduce | flops 1536 | bytes 6144
  65.2 37.2 %all_gather.27 = bf16[1,2,384]{1,0,2:T(2,128)(2,1)S(1)} all-gather(bf16[1,2,24]{1,0,2:T(2,128)(2,1)} %copy.130), channel_id=1, replica_groups=mesh['section'=2,'dp'=16] {'dp'}, dimensions={2}, use_global_device_ids=true | all-gather | bytes 1632 | tf_op jit(solution)/shard_map/all_gather | solution.py:207
  105.0 39.3 %all_gather.26 = bf16[1,2,384]{1,0,2:T(2,128)(2,1)S(1)} all-gather(bf16[1,2,24]{1,0,2:T(2,128)(2,1)} %copy.129), channel_id=1, replica_groups=mesh['section'=2,'dp'=16] {'dp'}, dimensions={2}, use_global_device_ids=true | all-gather | bytes 1632 | tf_op jit(solution)/shard_map/all_gather | solution.py:206
  146.7 40.0 %all_gather.29 = bf16[1,384,384]{2,1,0:T(8,128)(2,1)} all-gather(bf16[1,24,384]{2,1,0:T(8,128)(2,1)} %param.12), channel_id=1, replica_groups=mesh['section'=2,'dp'=16] {'dp'}, dimensions={1}, use_global_device_ids=true | all-gather | bytes 313344 | tf_op jit(solution)/shard_map/all_gather | solution.py:203
  186.7 42.7 %all_gather.28 = bf16[1,384,1152]{2,1,0:T(8,128)(2,1)S(1)} all-gather(bf16[1,24,1152]{2,1,0:T(8,128)(2,1)} %param.11), channel_id=1, replica_groups=mesh['section'=2,'dp'=16] {'dp'}, dimensions={1}, use_global_device_ids=true | all-gather | bytes 940032 | tf_op jit(solution)/shard_map/all_gather | solution.py:202
  238.1 11.4 %reshape.693 = bf16[6,256,3,6,64]{4,3,2,1,0:T(8,128)(2,1)} reshape(bf16[1536,1152]{1,0:T(8,128)(2,1)} %convolution_convert_fusion.2) | data formatting | bytes 7077888 | tf_op jit(solution)/shard_map/reshape | solution.py:71
  249.6 6.5 fusion.266
  259.3 4.7 copy.199
  267.3 6.4 fusion.270
  273.8 4.9 fusion.144
  282.1 26.1 %fusion.5 = (bf16[1536,1536]{1,0:T(8,128)(2,1)}, f32[1536,1536]{1,0:T(8,128)}) fusion(f32[1536]{0:T(1024)} %add.327, bf16[1,384,1536]{2,1,0:T(8,128)(2,1)} %all-gather.3.cloned.1.call-done, f32[1536,384]{1,0:T(8,128)S(1)} %get-tuple-element.67, f32[384]{0:T(512)} %get-tuple-element.34, f32[384]{0:T(512)} %get-tuple-element.32, ...), kind=kOutput, calls=%fused_computation.17 | convolution fusion | flops 1970601984 | bytes 17716224 | tf_op jit(solution)/shard_map/dot_general | solution.py:92
  308.3 6.4 fusion.80
  324.0 11.6 %reshape.694 = bf16[6,256,3,6,64]{4,3,2,1,0:T(8,128)(2,1)} reshape(bf16[1536,1152]{1,0:T(8,128)(2,1)} %convolution_convert_fusion.1) | data formatting | bytes 7077888 | tf_op jit(solution)/shard_map/reshape | solution.py:71
  335.5 6.5 fusion.265
  345.3 4.7 copy.202
  353.3 7.1 fusion.280
  360.4 4.9 fusion.138
  369.7 24.4 %fusion.8 = (bf16[1536,1536]{1,0:T(8,128)(2,1)S(1)}, f32[1536,1536]{1,0:T(8,128)}) fusion(f32[1536]{0:T(1024)S(1)} %copy-done.127, bf16[1,384,1536]{2,1,0:T(8,128)(2,1)S(1)} %copy-done.146, f32[1536,384]{1,0:T(8,128)S(1)} %get-tuple-element.73, f32[1536]{0:T(1024)S(1)} %add_rsqrt_fusion.2, f32[1536]{0:T(1024)S(1)} %broadcast_multiply_fusion.15, ...), kind=kOutput, calls=%fused_computation.20 | convolution fusion | flops 1970601984 | bytes 17716224 | tf_op jit(solution)/shard_map/dot_general | solution.py:92
  409.8 11.8 %reshape.695 = bf16[6,256,3,6,64]{4,3,2,1,0:T(8,128)(2,1)} reshape(bf16[1536,1152]{1,0:T(8,128)(2,1)} %convolution_convert_fusion) | data formatting | bytes 7077888 | tf_op jit(solution)/shard_map/reshape | solution.py:71
  421.6 6.5 fusion.264
  440.0 9.1 %fusion.290 = (f32[6,6,256]{2,1,0:T(8,128)S(1)}, f32[6,6,256,256]{2,3,1,0:T(8,128)}) fusion(pred[256]{0:T(512)(128)(4,1)S(1)} %copy-done.141, bf16[6,256,1,6,64]{1,4,3,0,2:T(8,128)(2,1)S(1)} %copy.207, bf16[6,256,1,6,64]{1,4,3,0,2:T(8,128)(2,1)} %copy.206), kind=kOutput, calls=%fused_computation.394 | convolution fusion | flops 311427328 | bytes 11833600 | tf_op jit(solution)/shard_map/sub | solution.py:82
  449.0 5.0 fusion.135
  458.3 24.1 %fusion.23 = (bf16[1536,1536]{1,0:T(8,128)(2,1)}, f32[1536,1536]{1,0:T(8,128)S(1)}) fusion(f32[1536]{0:T(1024)S(1)} %copy-done.128, bf16[1,384,1536]{2,1,0:T(8,128)(2,1)S(1)} %copy-done.147, f32[1536,384]{1,0:T(8,128)S(1)} %get-tuple-element.80, f32[1536]{0:T(1024)S(1)} %add_rsqrt_fusion, f32[1536]{0:T(1024)S(1)} %broadcast_multiply_fusion.13, ...), kind=kOutput, calls=%fused_computation.35 | convolution fusion | flops 1970601984 | bytes 17716224 | tf_op jit(solution)/shard_map/dot_general | solution.py:92
  482.4 6.1 convert_reduce_fusion.2
  497.5 4.7 reshape.696
  506.4 6.7 fusion.120
  513.1 7.6 multiply_reduce_fusion.2
  520.8 11.1 %multiply_convert_fusion.2 = bf16[6,6,256,256]{2,3,1,0:T(8,128)(2,1)} fusion(f32[6,6,256,256]{2,3,1,0:T(8,128)} %get-tuple-element.83, f32[6,6,256]{2,1,0:T(8,128)} %get-tuple-element.82, f32[6,6,256,256]{2,3,1,0:T(8,128)} %get-tuple-element.78, f32[6,6,256]{2,1,0:T(8,128)} %copy-done.91), kind=kLoop, calls=%fused_computation.56 | loop fusion | flops 9437184 | bytes 23666688 | tf_op jit(solution)/shard_map/convert_element_type | solution.py:162
  531.8 5.4 multiply_bitcast_fusion.2
  547.1 5.3 fusion.90
  562.5 6.6 fusion.150
  577.6 6.3 convert_reduce_fusion.1
  596.2 6.4 fusion.117
  602.6 7.7 multiply_reduce_fusion.1
  610.3 11.2 %multiply_convert_fusion.1 = bf16[6,6,256,256]{2,3,1,0:T(8,128)(2,1)} fusion(f32[6,6,256,256]{2,3,1,0:T(8,128)} %get-tuple-element.87, f32[6,6,256]{2,1,0:T(8,128)} %get-tuple-element.86, f32[6,6,256,256]{2,3,1,0:T(8,128)} %get-tuple-element.71, f32[6,6,256]{2,1,0:T(8,128)} %get-tuple-element.70), kind=kLoop, calls=%fused_computation.54 | loop fusion | flops 9437184 | bytes 23666688 | tf_op jit(solution)/shard_map/convert_element_type | solution.py:162
  640.8 5.7 fusion.98
  664.8 6.8 convert_reduce_fusion
  683.9 6.4 fusion.141
  690.2 7.5 multiply_reduce_fusion
  697.7 11.0 %multiply_convert_fusion = bf16[6,6,256,256]{2,3,1,0:T(8,128)(2,1)} fusion(f32[6,6,256,256]{2,3,1,0:T(8,128)} %get-tuple-element.91, f32[6,6,256]{2,1,0:T(8,128)} %get-tuple-element.90, f32[6,6,256,256]{2,3,1,0:T(8,128)} %get-tuple-element.65, f32[6,6,256]{2,1,0:T(8,128)} %get-tuple-element.64), kind=kLoop, calls=%fused_computation.52 | loop fusion | flops 9437184 | bytes 23666688 | tf_op jit(solution)/shard_map/convert_element_type | solution.py:162
  728.6 5.4 multiply_reduce_fusion.4
  738.4 7.0 all-to-all-start.2
  745.5 6.8 fusion.82
  752.8 6.7 all-to-all-start.1
  771.3 15.8 %all-to-all-done.1 = bf16[16,1,96,384]{3,2,1,0:T(8,128)(2,1)} async-done(((bf16[16,1,96,384]{3,2,1,0:T(8,128)(2,1)}), bf16[16,1,96,384]{3,2,1,0:T(8,128)(2,1)}, u32[]{:S(2)}, u32[]{:S(2)}) %all-to-all-start.1) | async-done | bytes 1179680 | tf_op jit(solution)/shard_map/all_to_all | solution.py:32
  787.1 7.3 all-to-all-start
  794.5 6.2 fusion.66
  810.6 31.3 %all-to-all-done = bf16[16,1,24,3072]{3,2,1,0:T(8,128)(2,1)} async-done(((bf16[16,1,24,3072]{3,2,1,0:T(8,128)(2,1)}), bf16[16,1,24,3072]{3,2,1,0:T(8,128)(2,1)}, u32[]{:S(2)}, u32[]{:S(2)}) %all-to-all-start) | async-done | bytes 2359328 | tf_op jit(solution)/shard_map/all_to_all | solution.py:32
  (513 shorter events, 241.9 us)
Async XLA Ops:
  7.2 274.9 %all-gather.3.cloned.1.call-start = ((), (), s32[]{:S(2)}) async-start(), calls=%async_computation.4 | async-start | bytes 1253376 | tf_op jit(solution)/shard_map/all_gather | solution.py:204
  7.9 300.4 %all-gather.5.cloned.1.call-start = ((), (), s32[]{:S(2)}) async-start(), calls=%async_computation.5 | async-start | bytes 1253376 | tf_op jit(solution)/shard_map/all_gather | solution.py:205
  10.8 51.1 %copy-start.4 = (bf16[1,2,6,256,384]{4,3,2,1,0:T(8,128)(2,1)S(1)}, bf16[1,2,6,256,384]{4,3,2,1,0:T(8,128)(2,1)}, u32[]{:S(2)}) copy-start(bf16[1,2,6,256,384]{4,3,2,1,0:T(8,128)(2,1)} %param.9) | copy-start | bytes 7077892
  14.7 303.9 %copy-start.17 = (bf16[1,1,6,256,384]{4,3,2,1,0:T(8,128)(2,1)}, bf16[1,1,6,256,384]{4,3,2,1,0:T(8,128)(2,1)S(1)}, u32[]{:S(2)}) copy-start(bf16[1,1,6,256,384]{4,3,2,1,0:T(8,128)(2,1)S(1)} %get-tuple-element.55) | copy-start | bytes 3538948
  61.9 171.3 %copy-start.66 = (f32[6,256]{1,0:T(8,128)}, f32[6,256]{1,0:T(8,128)S(1)}, u32[]{:S(2)}) copy-start(f32[6,256]{1,0:T(8,128)S(1)} %broadcast_multiply_fusion.18) | copy-start | bytes 18436
  62.5 170.7 %copy-start.74 = (f32[6,256]{1,0:T(8,128)}, f32[6,256]{1,0:T(8,128)S(1)}, u32[]{:S(2)}) copy-start(f32[6,256]{1,0:T(8,128)S(1)} %add_rsqrt_fusion.5) | copy-start | bytes 18436
  65.2 165.5 %copy-start.139 = (pred[256]{0:T(512)(128)(4,1)S(1)}, pred[256]{0:T(512)(128)(4,1)}, u32[]{:S(2)}) copy-start(pred[256]{0:T(512)(128)(4,1)} %iota_compare_fusion) | copy-start | bytes 772
  105.0 128.2 %copy-start.120 = (f32[384]{0:T(512)}, f32[384]{0:T(512)S(1)}, u32[]{:S(2)}) copy-start(f32[384]{0:T(512)S(1)} %get-tuple-element.35) | copy-start | bytes 4612
  146.7 86.5 %copy-start.82 = (f32[384]{0:T(512)}, f32[384]{0:T(512)S(1)}, u32[]{:S(2)}) copy-start(f32[384]{0:T(512)S(1)} %get-tuple-element.33) | copy-start | bytes 4612
  259.3 8.0 copy-start.39
  281.5 26.7 %copy-start.7 = (f32[1536,384]{1,0:T(8,128)}, f32[1536,384]{1,0:T(8,128)S(1)}, u32[]{:S(2)}) copy-start(f32[1536,384]{1,0:T(8,128)S(1)} %get-tuple-element.67) | copy-start | bytes 7077892
  281.5 26.7 %copy-start.68 = (f32[1536]{0:T(1024)}, f32[1536]{0:T(1024)S(1)}, u32[]{:S(2)}) copy-start(f32[1536]{0:T(1024)S(1)} %broadcast_multiply_fusion.17) | copy-start | bytes 18436
  282.1 26.1 %copy-start.93 = (f32[1536]{0:T(1024)}, f32[1536]{0:T(1024)S(1)}, u32[]{:S(2)}) copy-start(f32[1536]{0:T(1024)S(1)} %add_rsqrt_fusion.4) | copy-start | bytes 18436
  308.3 7.8 copy-start.103
  314.7 4.0 collective-permute-start
  316.1 78.1 %copy-start.72 = (f32[1536]{0:T(1024)}, f32[1536]{0:T(1024)S(1)}, u32[]{:S(2)}) copy-start(f32[1536]{0:T(1024)S(1)} %reshape.685) | copy-start | bytes 18436
  319.1 47.3 %copy-start.15 = (bf16[1536,384]{1,0:T(8,128)(2,1)}, bf16[1536,384]{1,0:T(8,128)(2,1)S(1)}, u32[]{:S(2)}) copy-start(bf16[1536,384]{1,0:T(8,128)(2,1)S(1)} %get-tuple-element.41) | copy-start | bytes 3538948
  345.3 8.0 copy-start.40
  367.5 26.6 %copy-start.12 = (f32[1536,384]{1,0:T(8,128)}, f32[1536,384]{1,0:T(8,128)S(1)}, u32[]{:S(2)}) copy-start(f32[1536,384]{1,0:T(8,128)S(1)} %get-tuple-element.73) | copy-start | bytes 7077892
  367.6 26.5 %copy-start.70 = (f32[1536]{0:T(1024)}, f32[1536]{0:T(1024)S(1)}, u32[]{:S(2)}) copy-start(f32[1536]{0:T(1024)S(1)} %broadcast_multiply_fusion.15) | copy-start | bytes 18436
  369.7 24.4 %copy-start.100 = (f32[1536]{0:T(1024)}, f32[1536]{0:T(1024)S(1)}, u32[]{:S(2)}) copy-start(f32[1536]{0:T(1024)S(1)} %add_rsqrt_fusion.2) | copy-start | bytes 18436
  369.7 24.5 %copy-start.142 = (bf16[1,1536,384]{2,1,0:T(8,128)(2,1)S(1)}, bf16[1,1536,384]{2,1,0:T(8,128)(2,1)}, u32[]{:S(2)}) copy-start(bf16[1,1536,384]{2,1,0:T(8,128)(2,1)} %all-gather.5.cloned.1.call-done) | copy-start | bytes 3538948
  394.2 8.0 copy-start.67
  394.2 8.5 %copy-start.75 = (f32[6,256]{1,0:T(8,128)S(1)}, f32[6,256]{1,0:T(8,128)}, u32[]{:S(2)}) copy-start(f32[6,256]{1,0:T(8,128)} %copy-done.74) | copy-start | bytes 18436
  394.2 9.1 %copy-start.77 = (f32[6,256]{1,0:T(8,128)S(1)}, f32[6,256]{1,0:T(8,128)}, u32[]{:S(2)}) copy-start(f32[6,256]{1,0:T(8,128)} %copy-done.76) | copy-start | bytes 18436
  394.2 9.7 %copy-start.18 = (bf16[1,1,6,256,384]{4,3,2,1,0:T(8,128)(2,1)S(1)}, bf16[1,1,6,256,384]{4,3,2,1,0:T(8,128)(2,1)}, u32[]{:S(2)}) copy-start(bf16[1,1,6,256,384]{4,3,2,1,0:T(8,128)(2,1)} %copy-done.17) | copy-start | bytes 3538948
  398.8 5.1 collective-permute-start.1
  439.9 9.1 %copy-start.37 = (bf16[6,256,1,6,64]{1,4,3,0,2:T(8,128)(2,1)}, bf16[6,256,1,6,64]{1,4,3,0,2:T(8,128)(2,1)S(1)}, u32[]{:S(2)}) copy-start(bf16[6,256,1,6,64]{1,4,3,0,2:T(8,128)(2,1)S(1)} %copy.207) | copy-start | bytes 3538948
  456.2 36.1 %copy-start.10 = (f32[1536,384]{1,0:T(8,128)}, f32[1536,384]{1,0:T(8,128)S(1)}, u32[]{:S(2)}) copy-start(f32[1536,384]{1,0:T(8,128)S(1)} %get-tuple-element.80) | copy-start | bytes 7077892
  458.3 33.9 %copy-start.113 = (f32[1536]{0:T(1024)}, f32[1536]{0:T(1024)S(1)}, u32[]{:S(2)}) copy-start(f32[1536]{0:T(1024)S(1)} %add_rsqrt_fusion) | copy-start | bytes 18436
  458.3 24.1 %copy-start.55 = (bf16[1,1,6,256,384]{4,3,2,1,0:T(8,128)(2,1)S(1)}, bf16[1,1,6,256,384]{4,3,2,1,0:T(8,128)(2,1)}, u32[]{:S(2)}) copy-start(bf16[1,1,6,256,384]{4,3,2,1,0:T(8,128)(2,1)} %get-tuple-element.56) | copy-start | bytes 3538948
  458.3 24.1 %copy-start.143 = (bf16[1,1536,384]{2,1,0:T(8,128)(2,1)S(1)}, bf16[1,1536,384]{2,1,0:T(8,128)(2,1)}, u32[]{:S(2)}) copy-start(bf16[1,1536,384]{2,1,0:T(8,128)(2,1)} %all-gather.5.cloned.1.call-done) | copy-start | bytes 3538948
  557.7 15.0 %slice-start.6 = ((s8[4718592]{0:T(1024)(128)(4,1)}), s8[4194304]{0:T(1024)(128)(4,1)S(1)}, s32[]{:S(2)}) async-start(s8[4718592]{0:T(1024)(128)(4,1)} %bitcast.392), calls=%async_computation.12 | async-start | bytes 8388608
  560.7 15.5 %collective-permute-start.2 = (bf16[1536,384]{1,0:T(8,128)(2,1)S(1)}, bf16[1536,384]{1,0:T(8,128)(2,1)S(1)}, u32[]{:S(2)}, u32[]{:S(2)}) collective-permute-start(bf16[1536,384]{1,0:T(8,128)(2,1)S(1)} %fusion.89), channel_id=1, source_target_pairs={{16,0},{17,1},{18,2},{19,3},{20,4},{21,5},{22,6},{23,7},{24,8},{25... | collective-permute-start | bytes 3538952 | tf_op jit(solution)/shard_map/ppermute | solution.py:22
  562.5 10.1 %slice-start.7 = ((s8[4718592]{0:T(1024)(128)(4,1)}), s8[524288]{0:T(1024)(128)(4,1)S(1)}, s32[]{:S(2)}) async-start(s8[4718592]{0:T(1024)(128)(4,1)} %bitcast.392), calls=%async_computation.13 | async-start | bytes 1048576
  569.2 7.6 slice-start.8
  569.2 7.6 slice-start.9
  576.7 7.1 copy-start.57
  588.9 62.9 %copy-start.3 = (f32[1536,384]{1,0:T(8,128)}, f32[1536,384]{1,0:T(8,128)S(1)}, u32[]{:S(2)}) copy-start(f32[1536,384]{1,0:T(8,128)S(1)} %multiply_add_fusion.2) | copy-start | bytes 7077892
  656.0 8.7 %collective-permute-start.3 = (bf16[1536,384]{1,0:T(8,128)(2,1)S(1)}, bf16[1536,384]{1,0:T(8,128)(2,1)S(1)}, u32[]{:S(2)}, u32[]{:S(2)}) collective-permute-start(bf16[1536,384]{1,0:T(8,128)(2,1)S(1)} %get-tuple-element.36), channel_id=1, source_target_pairs={{16,0},{17,1},{18,2},{19,3},{20,4},{21,5},{22,6},{23,7},{24,8},{25... | collective-permute-start | bytes 3538952 | tf_op jit(solution)/shard_map/ppermute | solution.py:22
  664.7 10.5 %copy-start.49 = (bf16[1536,384]{1,0:T(8,128)(2,1)}, bf16[1536,384]{1,0:T(8,128)(2,1)S(1)}, u32[]{:S(2)}) copy-start(bf16[1536,384]{1,0:T(8,128)(2,1)S(1)} %collective-permute-done.3) | copy-start | bytes 3538948
  715.8 22.6 %all-to-all-start.3 = ((bf16[16,1,96]{2,1,0:T(2,128)(2,1)}), bf16[16,1,96]{2,1,0:T(2,128)(2,1)}, u32[]{:S(2)}, u32[]{:S(2)}) async-start(bf16[16,1,96]{2,1,0:T(2,128)(2,1)} %convert_element_type.432), calls=%async_computation.3 | async-start | bytes 16384 | tf_op jit(solution)/shard_map/all_to_all | solution.py:32
  728.6 16.8 %copy-start.50 = (bf16[1536,384]{1,0:T(8,128)(2,1)S(1)}, bf16[1536,384]{1,0:T(8,128)(2,1)}, u32[]{:S(2)}) copy-start(bf16[1536,384]{1,0:T(8,128)(2,1)} %copy-done.49) | copy-start | bytes 3538948
  738.4 14.4 %all-to-all-start.2 = ((bf16[16,2,2,24]{3,2,1,0:T(2,128)(2,1)}), bf16[16,2,2,24]{3,2,1,0:T(2,128)(2,1)}, u32[]{:S(2)}, u32[]{:S(2)}) async-start(bf16[16,2,2,24]{3,2,1,0:T(2,128)(2,1)} %maximum_bitcast_fusion), calls=%async_computation.2 | async-start | bytes 32768 | tf_op jit(solution)/shard_map/all_to_all | solution.py:32
  752.3 7.3 copy-start.28
  752.8 34.3 %all-to-all-start.1 = ((bf16[16,1,96,384]{3,2,1,0:T(8,128)(2,1)}), bf16[16,1,96,384]{3,2,1,0:T(8,128)(2,1)}, u32[]{:S(2)}, u32[]{:S(2)}) async-start(bf16[16,1,96,384]{3,2,1,0:T(8,128)(2,1)} %bitcast.374), calls=%async_computation.1 | async-start | bytes 2359296 | tf_op jit(solution)/shard_map/all_to_all | solution.py:32
  771.3 23.1 %copy-start.106 = (f32[1536]{0:T(1024)S(1)}, f32[1536]{0:T(1024)}, u32[]{:S(2)}) copy-start(f32[1536]{0:T(1024)} %reshape.681) | copy-start | bytes 18436
  787.1 54.8 %all-to-all-start = ((bf16[16,1,24,3072]{3,2,1,0:T(8,128)(2,1)}), bf16[16,1,24,3072]{3,2,1,0:T(8,128)(2,1)}, u32[]{:S(2)}, u32[]{:S(2)}) async-start(bf16[16,1,24,3072]{3,2,1,0:T(8,128)(2,1)} %pad_maximum_fusion.1), calls=%async_computation | async-start | bytes 4718592 | tf_op jit(solution)/shard_map/all_to_all | solution.py:32
  (136 other events, 509.3 us)
Sparse Core Ops, SparseCore 0:
  10.8 58.7 all-gather.2
  72.4 55.5 all-gather.4
where the time goes:
time: 866 us; the launch traced here: 853 us
  matrix products  297 us (34%)
  blocking collectives  203 us (23%)
  local copies, waits for them, and re-layouts  165 us (19%)
  other arithmetic  86.3 us (10%)
  waiting for transfers between devices  51.7 us (6%)
  starting transfers between devices  33.3 us (4%)
  between operations  17.3 us (2%)
    dot_general x3, matrix products, run_layer(): jnp.dot(mid_low, w_up, preferred_element_type=jnp.float32)  74.6 us
    unnamed x368, local copies, waits for them, and re-layouts  55.5 us
    all_to_all x4, waiting for transfers between devices, sum_at_owner(): lax.all_to_all(parts, axis, split_axis=0, concat_axis=0, tiled=True)  47.7 us
    unnamed x1, blocking collectives  43.8 us
    all_gather x1, blocking collectives, body(): lax.all_gather(qkv_weight, 'dp', axis=1, tiled=True)  42.7 us
    all_gather x1, blocking collectives, body(): lax.all_gather(out_weight, 'dp', axis=1, tiled=True)  40 us
    all_gather x1, blocking collectives, body(): lax.all_gather(norm_gains, 'dp', axis=2, tiled=True)  39.3 us
    all_gather x1, blocking collectives, body(): lax.all_gather(norm_shifts, 'dp', axis=2, tiled=True)  37.2 us
  transfers between devices with their start and end apart: 10, of which 4 were waited for; matrix products, arithmetic and copies ran while one was open for 19% of the time, Pallas kernels for 0%

commit v1 on v0

v1 whole, which is shorter than its diff:
```python
import functools
import math

import jax, jax.numpy as jnp
from jax import lax
from jax.experimental import pallas as pl
from jax.experimental.pallas import tpu as pltpu
from jax.sharding import PartitionSpec as P

D = 384; H = 6; HD = 64; FF = 1536; PAD = 256; SEQ = 197
R = 208
EPS = 1e-06
SQRT_HALF = 0.7071067811865476
INV_ROOT_TWO_PI = 0.3989422804014327
F32 = jnp.float32; BF = jnp.bfloat16

def nn(a, b):
    return jnp.dot(a, b, preferred_element_type=F32)
def nt(a, b):
    return lax.dot_general(a, b, (((1,), (1,)), ((), ())), preferred_element_type=F32)
def tn(a, b):
    return lax.dot_general(a, b, (((0,), (0,)), ((), ())), preferred_element_type=F32)

def unit(v):
    c = v - jnp.mean(v, -1, keepdims=True)
    r = lax.rsqrt(jnp.mean(c * c, -1, keepdims=True) + EPS)
    return c * r, r

def low_half():
    return lax.broadcasted_iota(jnp.int32, (1, 128), 1) < HD

def fwd_attn(x, W, S, i):
    z, _ = unit(x)
    n1 = (z * W['g'][0:1] + W['c'][0:1]).astype(BF)
    S['n1'][i] = n1
    S['qkv'][i, 0:R] = nn(n1, W['qkv'][...]).astype(BF)
    half = low_half()
    real = lax.broadcasted_iota(jnp.int32, (1, PAD), 1) < SEQ
    for p in range(H // 2):
        a = p * 128
        q = S['qkv'][i, 0:R, a:a + 128]
        k = S['qkv'][i, :, D + a:D + a + 128]
        v = S['qkv'][i, :, 2 * D + a:2 * D + a + 128]
        qs = q * jnp.asarray(0.125, BF)
        zero = jnp.zeros_like(qs)
        outs, rls = [], []
        for h in range(2):
            qm = jnp.where(half if h == 0 else ~half, qs, zero)
            s = jnp.where(real, nt(qm, k), -1e30)
            e = jnp.exp(s - jnp.max(s, -1, keepdims=True))
            l = jnp.sum(e, -1, keepdims=True)
            eb = e.astype(BF)
            S['E'][i, (2 * p + h) * R:(2 * p + h + 1) * R] = eb
            outs.append(nn(eb, v)); rls.append(1.0 / l)
        rl = jnp.where(half, rls[0], rls[1])
        S['rl'][i, :, a:a + 128] = rl
        S['att'][i, :, a:a + 128] = (jnp.where(half, outs[0], outs[1]) * rl).astype(BF)
    S['mid'][i] = x + nn(S['att'][i], W['out'][...])

CH = 256
def fwd_mlp(W, S, i):
    mid = S['mid'][i]
    z, _ = unit(mid)
    n2 = (z * W['g'][1:2] + W['c'][1:2]).astype(BF)
    S['n2'][i] = n2
    for j in range(FF // CH):
        sl = slice(j * CH, (j + 1) * CH)
        u = nn(n2, W['up'][:, sl]) + W['ub'][0:1, sl]
        phi = 0.5 * (1.0 + lax.erf(u * SQRT_HALF))
        S['f'][i, :, sl] = (u * phi).astype(BF)
        S['sl'][i, :, sl] = (phi + u * (jnp.exp(-0.5 * u * u) * INV_ROOT_TWO_PI)).astype(BF)
    return mid + nn(S['f'][i], W['down'][...])

def norm_back(g_out, z, r, gain):
    t = g_out * gain
    gi = r * (t - jnp.mean(t, -1, keepdims=True) - z * jnp.mean(t * z, -1, keepdims=True))
    return gi, jnp.sum(g_out * z, 0, keepdims=True), jnp.sum(g_out, 0, keepdims=True)

def bwd_mlp(gm, W, S, i, G):
    G['down'][...] += tn(S['f'][i], gm)
    for j in range(FF // CH):
        sl = slice(j * CH, (j + 1) * CH)
        gu = (nt(gm, W['down'][sl, :]) * S['sl'][i, :, sl].astype(F32)).astype(BF)
        S['gu'][:, sl] = gu
        G['ub'][0:1, sl] += jnp.sum(gu.astype(F32), 0, keepdims=True)
    gu = S['gu'][...]
    G['up'][...] += tn(S['n2'][i], gu)
    gn = nt(gu, W['up'][...])
    z, r = unit(S['mid'][i])
    gi, dg, dc = norm_back(gn, z, r, W['g'][1:2])
    G['g'][1:2] += dg
    G['c'][1:2] += dc
    S['gmid'][i] = gm.astype(F32) + gi

def bwd_attn(x, W, S, i, G):
    gmid = S['gmid'][i]
    ga = gmid.astype(BF)
    att_all = S['att'][i]
    G['out'][...] += tn(att_all, ga)
    S['gatt'][...] = nt(ga, W['out'][...]).astype(BF)
    half = low_half()
    for p in range(H // 2):
        a = p * 128
        k = S['qkv'][i, :, D + a:D + a + 128]
        v = S['qkv'][i, :, 2 * D + a:2 * D + a + 128]
        qs = S['qkv'][i, 0:R, a:a + 128] * jnp.asarray(0.125, BF)
        gat = S['gatt'][:, a:a + 128].astype(F32) * S['rl'][i, :, a:a + 128]
        prod = gat * S['att'][i, :, a:a + 128].astype(F32)
        gatb = gat.astype(BF)
        gq = gk = gv = None
        for h in range(2):
            hm = half if h == 0 else ~half
            d = jnp.sum(jnp.where(hm, prod, 0.0), -1, keepdims=True)
            gm = jnp.where(hm, gatb, jnp.zeros_like(gatb))
            eb = S['E'][i, (2 * p + h) * R:(2 * p + h + 1) * R]
            gs = (eb.astype(F32) * (nt(gm, v) - d)).astype(BF)
            gvh = tn(eb, gm)
            gqh = nn(gs, jnp.where(hm, k, jnp.zeros_like(k)))
            gkh = tn(gs, jnp.where(hm, qs, jnp.zeros_like(qs)))
            if h == 0:
                gq, gk, gv = gqh, gkh, gvh
            else:
                gq, gk, gv = gq + gqh, gk + gkh, gv + gvh
        S['gqkv'][:, a:a + 128] = (gq * 0.125).astype(BF)
        S['gqkv'][:, D + a:D + a + 128] = gk[0:R].astype(BF)
        S['gqkv'][:, 2 * D + a:2 * D + a + 128] = gv[0:R].astype(BF)
    gqkv = S['gqkv'][...]
    G['qkv'][...] += tn(S['n1'][i], gqkv)
    gn = nt(gqkv, W['qkv'][...])
    z, r = unit(x)
    gi, dg, dc = norm_back(gn, z, r, W['g'][0:1])
    G['g'][0:1] += dg
    G['c'][0:1] += dc
    return gmid + gi
N = 6
STATE = dict(n1=((R, D), BF), qkv=((PAD, 3 * D), BF), E=((H * R, PAD), BF), rl=((R, D), F32), att=((R, D), BF),
             mid=((R, D), F32), n2=((R, D), BF), f=((R, FF), BF), sl=((R, FF), BF), gmid=((R, D), F32))
SHARED = dict(gu=((R, FF), BF), gatt=((R, D), BF), gqkv=((R, 3 * D), BF))
def scratch():
    out, names = [], []
    for L, n in ((0, N), (1, 1)):
        for k, (s, t) in STATE.items():
            out.append(pltpu.VMEM((n,) + s, t)); names.append((L, k))
    for k, (s, t) in SHARED.items():
        out.append(pltpu.VMEM(s, t)); names.append((2, k))
    out.append(pltpu.VMEM((N, R, D), BF)); names.append((2, 'x1'))
    out.append(pltpu.VMEM((N, R, D), BF)); names.append((2, 'gy'))
    return out, names

def kern(stages, x_ref, g_ref, wqkv, wout, wup, wdown, gg, cc, ub, out_ref, gin_ref, dqkv, dout, dup, ddown, dg, dc, dub, *sc):
    _, names = scratch()
    S = [{}, {}]
    for (L, k), ref in zip(names, sc):
        for l in ((0, 1) if L == 2 else (L,)):
            S[l][k] = ref
    W = [dict(qkv=wqkv.at[l], out=wout.at[l], up=wup.at[l], down=wdown.at[l], g=gg.at[l], c=cc.at[l], ub=ub.at[l]) for l in range(2)]
    G = [dict(qkv=dqkv.at[l], out=dout.at[l], up=dup.at[l], down=ddown.at[l], g=dg.at[l], c=dc.at[l], ub=dub.at[l]) for l in range(2)]
    for r in (dqkv, dout, dup, ddown, dg, dc, dub):
        r[...] = jnp.zeros_like(r)
    for l in range(2):
        for i in range(N if l == 0 else 1):
            S[l]['qkv'][i, R:PAD] = jnp.zeros((PAD - R, 3 * D), BF)
    if 'z' in stages:
        out_ref[...] = jnp.zeros_like(out_ref); gin_ref[...] = jnp.zeros_like(gin_ref)
    def loop(name, f):
        if name in stages:
            lax.fori_loop(0, N, lambda i, c: (f(i), c)[1], 0)
    def f0a(i): fwd_attn(x_ref[i].astype(F32), W[0], S[0], i)
    def f0b(i): S[0]['x1'][i] = fwd_mlp(W[0], S[0], i).astype(BF)
    def fb1a(i):
        x = S[0]['x1'][i].astype(F32)
        fwd_attn(x, W[1], S[1], 0)
    def fb1b(i):
        out_ref[i, 0:R] = fwd_mlp(W[1], S[1], 0)
    def fb1c(i):
        bwd_mlp(g_ref[i], W[1], S[1], 0, G[1])
    def fb1d(i):
        x = S[0]['x1'][i].astype(F32)
        S[0]['gy'][i] = bwd_attn(x, W[1], S[1], 0, G[1]).astype(BF)
    def b0a(i): bwd_mlp(S[0]['gy'][i], W[0], S[0], i, G[0])
    def b0b(i): gin_ref[i, 0:R] = bwd_attn(x_ref[i].astype(F32), W[0], S[0], i, G[0])
    loop('a', f0a); loop('b', f0b)
    if 'F' in stages:
        def fb(i):
            fb1a(i); fb1b(i); fb1c(i); fb1d(i)
        lax.fori_loop(0, N, lambda i, c: (fb(i), c)[1], 0)
    loop('c', b0a); loop('d', b0b)

def call(stages='zabFcd'):
    sc, _ = scratch()
    f = jax.ShapeDtypeStruct
    outs = (f((N, PAD, D), F32), f((N, PAD, D), F32), f((2, D, 3 * D), F32), f((2, D, D), F32), f((2, D, FF), F32), f((2, FF, D), F32),
            f((2, 2, D), F32), f((2, 2, D), F32), f((2, 1, FF), F32))
    return pl.pallas_call(functools.partial(kern, stages), out_shape=outs,
        in_specs=[pl.BlockSpec(memory_space=pltpu.VMEM)] * 9, out_specs=tuple([pl.BlockSpec(memory_space=pltpu.VMEM)] * 9),
        scratch_shapes=sc, compiler_params=pltpu.CompilerParams(vmem_limit_bytes=67043328), name='compute_' + stages)


def swap(v):
    return lax.ppermute(v, "section", [(0, 1), (1, 0)])


def body(ends, counts, qkv_weight, out_weight, up_weight, down_weight, norm_gains, norm_shifts, up_bias):
    first = lax.axis_index("section") == 0
    n = lax.axis_size("dp")
    rows = qkv_weight.shape[1]
    wide = jnp.concatenate([qkv_weight[0], out_weight[0], up_weight[0]], 1)
    small = jnp.concatenate([norm_gains.reshape(-1), norm_shifts.reshape(-1), up_bias.reshape(-1)])
    wide = lax.all_gather(wide, "dp", axis=0, tiled=True)
    down = lax.all_gather(down_weight[0], "dp", axis=0, tiled=True)
    small = lax.all_gather(small, "dp", axis=0)
    def both(v):
        o = swap(v)
        return jnp.where(first, jnp.stack([v, o]), jnp.stack([o, v]))
    wide, down, small = both(wide), both(down), both(small)
    gains = small[:, :, :2 * rows].reshape(2, n, 2, rows).transpose(0, 2, 1, 3).reshape(2, 2, D).astype(F32)
    shifts = small[:, :, 2 * rows:4 * rows].reshape(2, n, 2, rows).transpose(0, 2, 1, 3).reshape(2, 2, D).astype(F32)
    ub = small[:, :, 4 * rows:].reshape(2, 1, FF).astype(F32)
    theirs = swap(jnp.where(first, ends[0, 1], ends[0, 0]))
    x = jnp.where(first, ends[0, 0], theirs)
    g = jnp.where(first, theirs, ends[0, 1])
    mine = jnp.where(first, counts[0, 0], counts[1, 0])
    live = ((lax.iota(jnp.int32, N)[:, None] < mine) & (lax.iota(jnp.int32, PAD)[None, :] < SEQ))[:, :, None]
    g = jnp.where(live, g, 0)[:, :R]
    res = call()(x[:, :R], g, wide[:, :, :3 * D], wide[:, :, 3 * D:4 * D], wide[:, :, 4 * D:], down, gains, shifts, ub)
    out = jnp.where(live, res[0], 0.0)
    gin = res[1]
    other = swap(jnp.where(first, out, gin))
    ends_out = jnp.where(first, jnp.stack([gin, other]), jnp.stack([other, out]))[None]

    def pair(v):
        own = jnp.where(first, v[0], v[1])
        o = swap(jnp.where(first, v[1], v[0]).astype(BF))
        return (own + o.astype(F32)).astype(BF)

    def owner(v):
        v = v.reshape(n, v.shape[0] // n, v.shape[1])
        return lax.all_to_all(v, "dp", 0, 0, tiled=True).astype(F32).sum(0)
    gw = owner(pair(jnp.concatenate(res[2:5], 2)))
    gd = owner(pair(res[5]))
    gs = jnp.concatenate([v.reshape(2, 2, n, rows).transpose(0, 2, 1, 3).reshape(2, n, 2 * rows) for v in res[6:8]] + [res[8].reshape(2, n, 4 * rows)], 2)
    gs = owner(pair(gs))[0]
    return (ends_out, gw[None, :, :3 * D], gw[None, :, 3 * D:4 * D], gw[None, :, 4 * D:], gd[None],
            gs[:2 * rows].reshape(1, 2, rows), gs[2 * rows:4 * rows].reshape(1, 2, rows), gs[4 * rows:][None])


def solution(mesh):
    w = P("section", "dp", None)
    io = P("section", None, "dp", None, None)
    nrm = P("section", None, "dp")
    return jax.shard_map(body, mesh=mesh, in_specs=(io, P(None, "dp"), w, w, w, w, nrm, nrm, P("section", "dp")),
                         out_specs=(io, w, w, w, w, nrm, nrm, P("section", "dp")), check_vma=False)
```

time: 866 us -> 377 us (0.44)
  matrix products: 297 us -> 0 us
  blocking collectives: 203 us -> 44.5 us
  local copies, waits for them, and re-layouts: 165 us -> 31.6 us
  Pallas kernels: 0 us -> 91.1 us
  waiting for transfers between devices: 51.7 us -> 129 us
  other arithmetic: 86.3 us -> 43.7 us
  starting transfers between devices: 33.3 us -> 15.7 us
    dot_general x51 -> x0, matrix products: 274 us -> none  [the longest x3 74.6 us: run_layer(): jnp.dot(mid_low, w_up, preferred_element_type=jnp.float32)]
    all_gather x4 -> x0, blocking collectives: 159 us -> none  [the longest x1 42.7 us: body(): lax.all_gather(qkv_weight, 'dp', axis=1, tiled=True)]
    pallas_call x0 -> x1, Pallas kernels: none -> 91.1 us  [body(): call()]
    all_gather x2, waiting for transfers between devices: 0.04 us -> 68 us  [the longest x1 50.1 us: body(): down = lax.all_gather(down_weight[0], 'dp', axis=0, tiled=True)]
    reshape x9 -> x10, local copies, waits for them, and re-layouts: 56.6 us -> 9.15 us  [the longest x4 5.08 us: body(): v.reshape(2, 2, n, rows).transpose(0, 2, 1, 3).reshape(2, n, 2 * rows)]
    unnamed x368 -> x29, local copies, waits for them, and re-layouts: 55.5 us -> 8.48 us
    convert_element_type x15 -> x7, other arithmetic: 49.4 us -> 15.3 us  [the longest x2 11.2 us: pair(): return (own + o.astype(F32)).astype(BF)]
    sub x3 -> x0, matrix products: 22.6 us -> none  [run_layer(): shifted = jnp.exp(scores - jnp.max(scores, -1, keepdims=True))]
  transfers between devices with their start and end apart: 10 -> 13, of which waited for: 4 -> 7; matrix products, arithmetic and copies ran while one was open for 19% -> 12% of each run, Pallas kernels for 0% -> 0%
where the time goes in v1:
time: 377 us; the launch traced here: 371 us
  waiting for transfers between devices  129 us (34%)
  Pallas kernels  91.1 us (24%)
  blocking collectives  44.5 us (12%)
  other arithmetic  43.7 us (12%)
  local copies, waits for them, and re-layouts  31.6 us (8%)
  between operations  16.2 us (4%)
  starting transfers between devices  15.7 us (4%)
    pallas_call x1, Pallas kernels, body(): call()  91.1 us
    all_to_all x3, waiting for transfers between devices, owner(): return lax.all_to_all(v, 'dp', 0, 0, tiled=True).astype(F32).sum(0)  53 us
    all_gather x1, waiting for transfers between devices, body(): down = lax.all_gather(down_weight[0], 'dp', axis=0, tiled=True)  50.1 us
    unnamed x1, blocking collectives  44.5 us
    all_gather x1, waiting for transfers between devices, body(): wide = lax.all_gather(wide, 'dp', axis=0, tiled=True)  17.9 us
    all_to_all x3, starting transfers between devices, owner(): return lax.all_to_all(v, 'dp', 0, 0, tiled=True).astype(F32).sum(0)  14.1 us
    convert_element_type x2, other arithmetic, pair(): return (own + o.astype(F32)).astype(BF)  11.2 us
    unnamed x29, local copies, waits for them, and re-layouts  8.48 us
  transfers between devices with their start and end apart: 13, of which 7 were waited for; matrix products, arithmetic and copies ran while one was open for 12% of the time, Pallas kernels for 0%

profile of v1, /device:TPU:0, one launch (start us, length us, event | category | flops | bytes accessed | tf_op | source)
XLA Modules:
  0.0 371.4 jit_solution(13213830029401061249)
XLA Ops:
  7.2 1.7 pad_maximum_fusion
  9.0 0.7 all-gather.7.cloned.1.call-update
  9.7 0.7 reshape.200
  10.5 0.7 reshape.201
  11.2 1.2 dynamic-slice
  13.1 0.7 pad_maximum_fusion.2
  14.1 44.5 %all-reduce = bf16[3072]{0:T(1024)(128)(2,1)S(1)} all-reduce(bf16[3072]{0:T(1024)(128)(2,1)S(1)} %dynamic-update-slice), channel_id=3, replica_groups=mesh['section'=2,'dp'=16] {'dp'}, use_global_device_ids=true, to_apply=%add | all-reduce | flops 3072 | bytes 12288
  58.7 17.9 %all-gather.5.cloned.1.call-done = bf16[384,3072]{1,0:T(8,128)(2,1)} async-done(((bf16[24,3072]{1,0:T(8,128)(2,1)}), bf16[384,3072]{1,0:T(8,128)(2,1)}) %all-gather.5.cloned.1.call-update) | async-done | bytes 2359312 | tf_op jit(solution)/shard_map/all_gather | solution.py:209
  76.6 2.8 broadcast_select_fusion
  82.3 1.3 slice_bitcast_fusion
  83.6 50.1 %all-gather.7.cloned.1.call-done = bf16[1,1536,384]{2,1,0:T(8,128)(2,1)} async-done(((bf16[1,96,384]{2,1,0:T(8,128)(2,1)}), bf16[1,1536,384]{2,1,0:T(8,128)(2,1)}) %all-gather.7.cloned.1.call-update) | async-done | bytes 1179664 | tf_op jit(solution)/shard_map/all_gather | solution.py:210
  133.7 0.7 broadcast_and_fusion
  134.5 0.8 maximum_select_fusion.3
  135.4 0.7 reshape.215.ub
  136.3 0.7 reshape.214.cc
  137.1 0.7 reshape.213.gg
  137.7 3.2 fusion.4
  141.0 1.8 maximum_select_fusion.2.wdown
  143.3 3.1 maximum_select_fusion
  146.4 0.9 slice.113.wout
  147.4 1.4 slice.112.wqkv
  148.7 1.6 slice.114.wup
  150.3 91.1 %compute_zabFcd.1 = (f32[6,256,384]{2,1,0:T(8,128)}, f32[6,256,384]{2,1,0:T(8,128)}, f32[2,384,1152]{2,1,0:T(8,128)}, f32[2,384,384]{2,1,0:T(8,128)}, f32[2,384,...) custom-call(bf16[6,208,384]{2,1,0:T(8,128)(2,1)} %get-tuple-element., ...), custom_call_target="tpu_custom_call" | custom-call | tf_op jit(solution)/shard_map/compute_zabFcd/pallas_call | solution.py:225
  241.4 0.9 reduce.1
  242.3 0.7 reshape.209
  243.0 1.4 reshape.205
  244.4 1.4 copy.27
  245.8 0.8 reshape.206
  246.6 1.4 reshape.207
  248.0 1.4 copy.28
  249.4 1.4 reshape.208
  250.8 3.6 fusion.3
  255.5 0.9 copy-done.5
  256.6 1.0 slice-done
  258.1 3.6 copy-done
  262.9 4.0 %collective-permute-done.7 = bf16[16,192]{1,0:T(8,128)(2,1)S(1)} collective-permute-done((bf16[16,192]{1,0:T(8,128)(2,1)S(1)}, bf16[16,192]{1,0:T(8,128)(2,1)S(1)}, u32[]{:S(2)}, u32[]{:S(2)}) %collective-permute-start.7) | collective-permute-done | bytes 6176 | tf_op jit(solution)/shard_map/ppermute | solution.py:200
  267.5 4.3 %all-to-all-start.2 = ((bf16[16,1,192]{2,1,0:T(2,128)(2,1)}), bf16[16,1,192]{2,1,0:T(2,128)(2,1)S(1)}, u32[]{:S(2)}, u32[]{:S(2)}) async-start(bf16[16,1,192]{2,1,0:T(2,128)(2,1)} %copy.29), calls=%async_computation.2 | async-start | bytes 32768 | tf_op jit(solution)/shard_map/all_to_all | solution.py:238
  271.8 4.1 %fusion.2 = bf16[1536,384]{1,0:T(8,128)(2,1)} fusion(bf16[1536,384]{1,0:T(8,128)(2,1)} %collective-permute-done.6, f32[2,1536,384]{2,1,0:T(8,128)} %get-tuple-element.22, pred[]{:T(512)S(6)} %eq.3), kind=kLoop, calls=%fused_computation.9 | loop fusion | flops 2359296 | bytes 7077889 | tf_op jit(solution)/shard_map/convert_element_type | solution.py:234
  275.9 3.3 all-to-all-done.2
  279.2 3.7 all-to-all-start.1
  282.9 7.1 %fusion = bf16[384,3072]{1,0:T(8,128)(2,1)} fusion(bf16[384,3072]{1,0:T(8,128)(2,1)} %collective-permute-done.5, f32[2,384,3072]{2,1,0:T(8,128)} %copy-done, pred[]{:T(512)S(6)} %eq.3), kind=kLoop, calls=%fused_computation.3 | loop fusion | flops 4718592 | bytes 14155777 | tf_op jit(solution)/shard_map/convert_element_type | solution.py:234
  290.0 19.5 %all-to-all-done.1 = bf16[16,96,384]{2,1,0:T(8,128)(2,1)S(1)} async-done(((bf16[16,96,384]{2,1,0:T(8,128)(2,1)}), bf16[16,96,384]{2,1,0:T(8,128)(2,1)S(1)}, u32[]{:S(2)}, u32[]{:S(2)}) %all-to-all-start.1) | async-done | bytes 1179680 | tf_op jit(solution)/shard_map/all_to_all | solution.py:238
  309.5 6.1 %all-to-all-start = ((bf16[16,24,3072]{2,1,0:T(8,128)(2,1)}), bf16[16,24,3072]{2,1,0:T(8,128)(2,1)S(1)}, u32[]{:S(2)}, u32[]{:S(2)}) async-start(bf16[16,24,3072]{2,1,0:T(8,128)(2,1)} %bitcast.69), calls=%async_computation | async-start | bytes 4718592 | tf_op jit(solution)/shard_map/all_to_all | solution.py:238
  315.6 4.2 %select_bitcast_fusion = (f32[1,1,6,256,384]{4,3,2,1,0:T(8,128)}, f32[6,256,384]{2,1,0:T(8,128)}) fusion(f32[6,256,384]{2,1,0:T(8,128)} %get-tuple-element.18, pred[6,256]{1,0:T(8,128)(4,1)} %copy-done.8, f32[6,256,384]{2,1,0:T(8,128)} %get-tuple-element.17, pred[]{:T(512)S(6)} %eq.3), kind=kLoop, calls=%fused_computation.12 | loop fusion | flops 1179648 | bytes 9438721 | tf_op jit(solution)/shard_map/stack | solution.py:229
  321.9 2.9 collective-permute-done.4
  324.7 6.4 %maximum_select_fusion.1 = f32[1,2,6,256,384]{4,3,2,1,0:T(8,128)} fusion(f32[1,1,6,256,384]{4,3,2,1,0:T(8,128)} %bitcast.17, f32[1,1,6,256,384]{4,3,2,1,0:T(8,128)} %bitcast.70, f32[1,1,6,256,384]{4,3,2,1,0:T(8,128)} %get-tuple-element.28, pred[]{:T(512)S(6)} %eq.3), kind=kLoop, calls=%fused_computation.1 | loop fusion | flops 3538944 | bytes 11796481 | tf_op jit(solution)/shard_map/jit(_where)/select_n | solution.py:229
  331.2 0.8 convert_reduce_fusion.1
  332.0 30.2 %all-to-all-done = bf16[16,24,3072]{2,1,0:T(8,128)(2,1)S(1)} async-done(((bf16[16,24,3072]{2,1,0:T(8,128)(2,1)}), bf16[16,24,3072]{2,1,0:T(8,128)(2,1)S(1)}, u32[]{:S(2)}, u32[]{:S(2)}) %all-to-all-start) | async-done | bytes 2359328 | tf_op jit(solution)/shard_map/all_to_all | solution.py:238
  (69 shorter events, 10.7 us)
Async XLA Ops:
  7.2 75.2 %copy-start.1 = (bf16[1,2,6,256,384]{4,3,2,1,0:T(8,128)(2,1)S(1)}, bf16[1,2,6,256,384]{4,3,2,1,0:T(8,128)(2,1)}, u32[]{:S(2)}) copy-start(bf16[1,2,6,256,384]{4,3,2,1,0:T(8,128)(2,1)} %param.9) | copy-start | bytes 7077892
  7.2 72.7 %copy-start.9 = (s32[2,1]{0,1:T(1,128)S(1)}, s32[2,1]{0,1:T(1,128)}, u32[]{:S(2)}) copy-start(s32[2,1]{0,1:T(1,128)} %param.10) | copy-start | bytes 28
  7.2 69.4 %all-gather.5.cloned.1.call-start = ((), (), s32[]{:S(2)}) async-start(), calls=%async_computation.3 | async-start | bytes 2506752 | tf_op jit(solution)/shard_map/all_gather | solution.py:209
  9.0 124.7 %all-gather.7.cloned.1.call-start = ((), (), s32[]{:S(2)}) async-start(), calls=%async_computation.4 | async-start | bytes 1253376 | tf_op jit(solution)/shard_map/all_gather | solution.py:210
  58.6 75.9 %collective-permute-start.3 = (bf16[16,192]{1,0:T(8,128)(2,1)S(1)}, bf16[16,192]{1,0:T(8,128)(2,1)}, u32[]{:S(2)}, u32[]{:S(2)}) collective-permute-start(bf16[16,192]{1,0:T(8,128)(2,1)S(1)} %reshape.219), channel_id=1, source_target_pairs={{0,16},{16,0},{1,17},{17,1},{2,18},{18,2},{3,19},{19,3},{4,20},{20... | collective-permute-start | bytes 18440 | tf_op jit(solution)/shard_map/ppermute | solution.py:200
  76.6 66.2 %collective-permute-start.1 = (bf16[384,3072]{1,0:T(8,128)(2,1)}, bf16[384,3072]{1,0:T(8,128)(2,1)}, u32[]{:S(2)}, u32[]{:S(2)}) collective-permute-start(bf16[384,3072]{1,0:T(8,128)(2,1)} %all-gather.5.cloned.1.call-done), channel_id=1, source_target_pairs={{0,16},{16,0},{1,17},{17,1},{2,18},{18,2},{3,19},{19,3},{4,20},{20... | collective-permute-start | bytes 7077896 | tf_op jit(solution)/shard_map/ppermute | solution.py:200
  79.4 58.3 %collective-permute-start = (bf16[6,256,384]{2,1,0:T(8,128)(2,1)}, bf16[6,256,384]{2,1,0:T(8,128)(2,1)}, u32[]{:S(2)}, u32[]{:S(2)}) collective-permute-start(bf16[6,256,384]{2,1,0:T(8,128)(2,1)} %broadcast_select_fusion), channel_id=1, source_target_pairs={{0,16},{16,0},{1,17},{17,1},{2,18},{18,2},{3,19},{19,3},{4,20},{20... | collective-permute-start | bytes 3538952 | tf_op jit(solution)/shard_map/ppermute | solution.py:200
  133.7 7.3 %collective-permute-start.2 = (bf16[1536,384]{1,0:T(8,128)(2,1)}, bf16[1536,384]{1,0:T(8,128)(2,1)S(1)}, u32[]{:S(2)}, u32[]{:S(2)}) collective-permute-start(bf16[1536,384]{1,0:T(8,128)(2,1)} %bitcast.74), channel_id=1, source_target_pairs={{0,16},{16,0},{1,17},{17,1},{2,18},{18,2},{3,19},{19,3},{4,20},{20... | collective-permute-start | bytes 3538952 | tf_op jit(solution)/shard_map/ppermute | solution.py:200
  134.4 6.5 %copy-start.8 = (pred[6,256]{1,0:T(8,128)(4,1)}, pred[6,256]{1,0:T(8,128)(4,1)S(1)}, u32[]{:S(2)}) copy-start(pred[6,256]{1,0:T(8,128)(4,1)S(1)} %broadcast_and_fusion) | copy-start | bytes 4612
  137.7 3.2 copy-start.4
  141.0 2.3 copy-start.3
  241.4 13.6 %copy-start.2 = (f32[2,384,1152]{2,1,0:T(8,128)S(1)}, f32[2,384,1152]{2,1,0:T(8,128)}, u32[]{:S(2)}) copy-start(f32[2,384,1152]{2,1,0:T(8,128)} %get-tuple-element.19) | copy-start | bytes 10616836
  254.5 17.4 %collective-permute-start.6 = (bf16[1536,384]{1,0:T(8,128)(2,1)}, bf16[1536,384]{1,0:T(8,128)(2,1)}, u32[]{:S(2)}, u32[]{:S(2)}) collective-permute-start(bf16[1536,384]{1,0:T(8,128)(2,1)} %fusion.3), channel_id=1, source_target_pairs={{0,16},{16,0},{1,17},{17,1},{2,18},{18,2},{3,19},{19,3},{4,20},{20... | collective-permute-start | bytes 3538952 | tf_op jit(solution)/shard_map/ppermute | solution.py:200
  255.0 2.5 slice-start
  255.0 1.4 copy-start.5
  255.0 2.7 slice-start.1
  258.1 3.6 copy-start
  261.7 0.7 copy-start.6
  261.7 0.7 copy-start.7
  262.1 20.7 %collective-permute-start.5 = (bf16[384,3072]{1,0:T(8,128)(2,1)S(1)}, bf16[384,3072]{1,0:T(8,128)(2,1)}, u32[]{:S(2)}, u32[]{:S(2)}) collective-permute-start(bf16[384,3072]{1,0:T(8,128)(2,1)S(1)} %fusion.1), channel_id=1, source_target_pairs={{0,16},{16,0},{1,17},{17,1},{2,18},{18,2},{3,19},{19,3},{4,20},{20... | collective-permute-start | bytes 7077896 | tf_op jit(solution)/shard_map/ppermute | solution.py:200
  262.6 4.3 %collective-permute-start.7 = (bf16[16,192]{1,0:T(8,128)(2,1)S(1)}, bf16[16,192]{1,0:T(8,128)(2,1)S(1)}, u32[]{:S(2)}, u32[]{:S(2)}) collective-permute-start(bf16[16,192]{1,0:T(8,128)(2,1)S(1)} %fusion.6), channel_id=1, source_target_pairs={{0,16},{16,0},{1,17},{17,1},{2,18},{18,2},{3,19},{19,3},{4,20},{20... | collective-permute-start | bytes 18440 | tf_op jit(solution)/shard_map/ppermute | solution.py:200
  267.5 11.7 %all-to-all-start.2 = ((bf16[16,1,192]{2,1,0:T(2,128)(2,1)}), bf16[16,1,192]{2,1,0:T(2,128)(2,1)S(1)}, u32[]{:S(2)}, u32[]{:S(2)}) async-start(bf16[16,1,192]{2,1,0:T(2,128)(2,1)} %copy.29), calls=%async_computation.2 | async-start | bytes 32768 | tf_op jit(solution)/shard_map/all_to_all | solution.py:238
  279.2 30.3 %all-to-all-start.1 = ((bf16[16,96,384]{2,1,0:T(8,128)(2,1)}), bf16[16,96,384]{2,1,0:T(8,128)(2,1)S(1)}, u32[]{:S(2)}, u32[]{:S(2)}) async-start(bf16[16,96,384]{2,1,0:T(8,128)(2,1)} %bitcast.27), calls=%async_computation.1 | async-start | bytes 2359296 | tf_op jit(solution)/shard_map/all_to_all | solution.py:238
  309.5 52.7 %all-to-all-start = ((bf16[16,24,3072]{2,1,0:T(8,128)(2,1)}), bf16[16,24,3072]{2,1,0:T(8,128)(2,1)S(1)}, u32[]{:S(2)}, u32[]{:S(2)}) async-start(bf16[16,24,3072]{2,1,0:T(8,128)(2,1)} %bitcast.69), calls=%async_computation | async-start | bytes 4718592 | tf_op jit(solution)/shard_map/all_to_all | solution.py:238
  319.9 4.9 %collective-permute-start.4 = (f32[6,256,384]{2,1,0:T(8,128)}, f32[6,256,384]{2,1,0:T(8,128)}, u32[]{:S(2)}, u32[]{:S(2)}) collective-permute-start(f32[6,256,384]{2,1,0:T(8,128)} %get-tuple-element.29), channel_id=1, source_target_pairs={{0,16},{16,0},{1,17},{17,1},{2,18},{18,2},{3,19},{19,3},{4,20},{20... | collective-permute-start | bytes 7077896 | tf_op jit(solution)/shard_map/ppermute | solution.py:200
Sparse Core Ops, SparseCore 0:
  11.4 65.1 all-gather.4
  79.4 54.2 all-gather.6
